TPU v7x, 256 devices: a 2x2x32 block of a 4x8x32 slice. The times are simulated.
256 devices in a mesh: groups: 4 (over x, y), expert: 32 (over z), mp: 2 (over core).
Axes of the slice: x: 2, y: 2, z: 32, core: 2. Of those that a mesh axis runs over, the one named last changes fastest.
The devices are a block of a 4x8x32 slice.
Arguments:
- residual: bfloat16 [4096, 5120], P(('groups', 'expert'), 'mp'), parts along dimension 0, may hold values from -6 to 6
- norm_gain: bfloat16 [5120], P('mp'), may hold values from 0.099609375 to 1.8984375
- router_weight: bfloat16 [640, 128], replicated, may hold values from -0.25 to 0.25
- expert_ids: int32 [4096, 8, 2], P(('groups', 'expert')), parts along dimension 0, may hold values from 0 to 127, all different within a row; in each aligned block of 256 rows (0 to 255, 256 to 511, ..., all dimensions but the last counted through in order) at most 5 rows name the same one
- expert_in: bfloat16 [128, 640, 1280], P('expert', None, 'mp'), may hold values from -0.25 to 0.25
- expert_out: bfloat16 [128, 1280, 640], P('expert', 'mp'), may hold values from -0.15625 to 0.15625
- queries: bfloat16 [4096, 5120], P(('groups', 'expert'), 'mp'), parts along dimension 0, may hold values from -6 to 6
- new_keys: bfloat16 [4096, 1024], P(('groups', 'expert'), 'mp'), parts along dimension 0, may hold values from -6 to 6
- new_values: bfloat16 [4096, 1024], P(('groups', 'expert'), 'mp'), parts along dimension 0, may hold values from -6 to 6
- cache_keys: bfloat16 [4096, 128, 1024], P(('groups', 'expert'), None, 'mp'), parts along dimension 0, may hold values from -6 to 6
- cache_values: bfloat16 [4096, 128, 1024], P(('groups', 'expert'), None, 'mp'), parts along dimension 0, may hold values from -6 to 6
- lengths: int32 [4096], P(('groups', 'expert')), parts along dimension 0, may hold values from 1 to 128
Outputs:
- attention: bfloat16 [4096, 5120], P(('groups', 'expert'), 'mp'), parts along dimension 0
- mixed: bfloat16 [4096, 5120], P(('groups', 'expert'), 'mp'), parts along dimension 0
There are 4 independent parts, one for each index of `groups`. A program takes and returns all parts, laid end to end along the dimension named above; an argument that names none is the same for every part. Nothing has to cross between parts.
Inputs may be any that keep to these rules, and one draw needn't show every extreme that they name: `expert_ids`: within the 8 sub-tokens of each aligned block of 32 tokens, no expert is named more than 5 times, a bound that some block reaches; the 2 experts of one sub-token differ.
All inputs are finite; a program needn't handle non-finite values.
Results may differ from a plain program's by a relative error of at most 0.006.
Values may be sent and summed in bfloat16 or wider, within the bound.
A program may use at most 128 MiB of HBM per device.

v0:
```python
import math

import jax
import jax.numpy as jnp
from jax import lax
from jax.sharding import PartitionSpec as P

D = 5120
SUB = 8
HEADS = 40
HD = 128
KV_HEADS = 8
EXPERTS = 128
TOP = 2
CAP = 5


def expert_ffn(received, first_weight, second_weight):
    hidden = jax.nn.gelu(
        jnp.einsum("scew,ewf->scef", received, first_weight, preferred_element_type=jnp.float32)
    ).astype(jnp.bfloat16)
    return jnp.einsum("scef,efw->scew", hidden, second_weight, preferred_element_type=jnp.float32)


def attend(queries, new_keys, new_values, cache_keys, cache_values, lengths):
    tokens = queries.shape[0]
    per_group = HEADS // KV_HEADS
    groups = new_keys.shape[1] // HD
    cache_len = cache_keys.shape[1]
    score_scale = 1.0 / math.sqrt(HD)
    query_heads = queries.reshape(tokens, groups, per_group, HD)
    keys_old = cache_keys.reshape(tokens, cache_len, groups, HD)
    values_old = cache_values.reshape(tokens, cache_len, groups, HD)
    keys_new = new_keys.reshape(tokens, groups, HD)
    values_new = new_values.reshape(tokens, groups, HD)
    scores = (
        jnp.einsum("tgqd,tjgd->tgqj", query_heads, keys_old, preferred_element_type=jnp.float32)
        * score_scale
    )
    fresh_score = (
        jnp.einsum("tgqd,tgd->tgq", query_heads, keys_new, preferred_element_type=jnp.float32)
        * score_scale
    )
    usable = (jnp.arange(cache_len, dtype=jnp.int32)[None, :] < lengths[:, None])[:, None, None, :]
    scores = jnp.where(usable, scores, -1e30)
    row_max = jnp.maximum(jnp.max(scores, axis=-1), fresh_score)
    expo_old = jnp.where(usable, jnp.exp(scores - row_max[..., None]), 0.0)
    expo_new = jnp.exp(fresh_score - row_max)
    totals = jnp.sum(expo_old, axis=-1) + expo_new
    cache_probs = (expo_old / totals[..., None]).astype(jnp.bfloat16)
    fresh_probs = (expo_new / totals).astype(jnp.bfloat16)
    context = jnp.einsum(
        "tgqj,tjgd->tgqd", cache_probs, values_old, preferred_element_type=jnp.float32
    )
    context = (
        context
        + fresh_probs.astype(jnp.float32)[..., None] * values_new.astype(jnp.float32)[:, :, None, :]
    )
    return context.reshape(tokens, groups * per_group * HD)


def per_device(
    residual,
    norm_gain,
    router_weight,
    expert_ids,
    expert_in,
    expert_out,
    queries,
    new_keys,
    new_values,
    cache_keys,
    cache_values,
    lengths,
):
    sub_width = D // SUB
    tokens = residual.shape[0]
    sub_local = residual.shape[1] // sub_width
    expert_count = lax.axis_size("expert")
    per_owner = expert_in.shape[0]
    pieces = residual.astype(jnp.float32).reshape(tokens, sub_local, sub_width)
    gain_rows = norm_gain.astype(jnp.float32).reshape(sub_local, sub_width)
    meansq = jnp.mean(pieces * pieces, axis=-1, keepdims=True)
    normed = (pieces * lax.rsqrt(meansq + 1e-06) * gain_rows).astype(jnp.bfloat16)
    own_ids = lax.dynamic_slice_in_dim(expert_ids, lax.axis_index("mp") * sub_local, sub_local, 1)
    logits = jnp.einsum("tsw,we->tse", normed, router_weight, preferred_element_type=jnp.float32)
    expert_range = jnp.arange(EXPERTS, dtype=jnp.int32)
    chosen = (own_ids[..., None] == expert_range).astype(jnp.float32)
    picked_logits = jnp.sum(chosen * logits[:, :, None, :], axis=-1)
    gate_scores = jax.nn.sigmoid(picked_logits)
    weights = gate_scores / jnp.sum(gate_scores, axis=-1, keepdims=True)
    flat_ids = own_ids.reshape(-1)
    choice_count = flat_ids.shape[0]
    onehot = (flat_ids[:, None] == expert_range[None, :]).astype(jnp.bfloat16)
    positions = jnp.arange(choice_count, dtype=jnp.int32)
    earlier = (positions[:, None] > positions[None, :]).astype(jnp.bfloat16)
    before = jnp.dot(earlier, onehot, preferred_element_type=jnp.float32)
    slot_index = jnp.sum(before * onehot.astype(jnp.float32), axis=1).astype(jnp.int32)
    owner_index = flat_ids // per_owner
    local_index = flat_ids % per_owner
    flat_index = (owner_index * CAP + slot_index) * per_owner + local_index
    dispatch = (flat_index[:, None] == jnp.arange(EXPERTS * CAP, dtype=jnp.int32)[None, :]).astype(
        jnp.bfloat16
    )
    sources = jnp.broadcast_to(normed[:, :, None, :], (tokens, sub_local, TOP, sub_width)).reshape(
        choice_count, sub_width
    )
    outgoing = jnp.einsum(
        "cs,cw->sw", dispatch, sources, preferred_element_type=jnp.float32
    ).astype(jnp.bfloat16)
    outgoing = outgoing.reshape(expert_count, CAP, per_owner, sub_width)
    full_in, full_out = (
        lax.all_gather(expert_in, "mp", axis=2, tiled=True),
        lax.all_gather(expert_out, "mp", axis=1, tiled=True),
    )
    result_rows = expert_ffn(
        lax.all_to_all(outgoing, "expert", split_axis=0, concat_axis=0, tiled=True),
        full_in,
        full_out,
    ).astype(jnp.bfloat16)
    returned = lax.all_to_all(result_rows, "expert", split_axis=0, concat_axis=0, tiled=True)
    picked = jnp.dot(
        dispatch, returned.reshape(EXPERTS * CAP, sub_width), preferred_element_type=jnp.float32
    )
    picked = picked.reshape(tokens, sub_local, TOP, sub_width)
    moe = jnp.sum(weights[..., None] * picked, axis=2).reshape(tokens, sub_local * sub_width)
    context = attend(queries, new_keys, new_values, cache_keys, cache_values, lengths)
    attention = context.astype(jnp.bfloat16)
    mixed = (residual.astype(jnp.float32) + context + moe).astype(jnp.bfloat16)
    return (attention, mixed)


def solution(mesh):
    placed = (
        P(("groups", "expert"), "mp"),
        P("mp"),
        P(),
        P(("groups", "expert"), None, None),
        P("expert", None, "mp"),
        P("expert", "mp", None),
        P(("groups", "expert"), "mp"),
        P(("groups", "expert"), "mp"),
        P(("groups", "expert"), "mp"),
        P(("groups", "expert"), None, "mp"),
        P(("groups", "expert"), None, "mp"),
        P(("groups", "expert")),
    )
    return jax.shard_map(
        per_device,
        mesh=mesh,
        in_specs=placed,
        out_specs=(P(("groups", "expert"), "mp"), P(("groups", "expert"), "mp")),
        check_vma=False,
    )
```

profile of v0, /device:TPU:37, one launch (start us, length us, event | category | flops | bytes accessed | tf_op | source)
XLA Modules:
  0.0 242.2 jit_solution(5904130037478334206)
XLA Ops:
  7.3 0.7 all-gather.3.cloned.1.call-update
  8.0 0.1 all-gather.5.cloned.1.call-start
  8.1 0.7 all-gather.5.cloned.1.call-update
  8.8 0.1 reshape.176
  9.0 0.1 multiply_reduce_fusion
  9.2 0.1 copy.74
  9.3 0.1 eq.68
  9.4 0.2 fusion.41
  9.7 0.1 multiply_convert_fusion
  9.8 0.2 broadcast_in_dim.19
  10.0 0.1 reshape.177
  10.2 0.6 convolution_convert_fusion
  10.8 0.2 reshape.178
  11.0 121.0 %all_to_all.10 = bf16[32,5,4,640]{3,2,1,0:T(4,128)(2,1)S(1)} all-to-all(bf16[32,5,4,640]{3,2,1,0:T(4,128)(2,1)S(1)} %reshape.178), channel_id=1, replica_groups=mesh['groups'=4,'expert'=32,'mp'=2] {'expert'}, dimensions={0} | all-to-all | bytes 1638400 | tf_op jit(solution)/shard_map/all_to_all | solution.py:117
  132.0 7.6 %fusion.28 = bf16[32,5,4,640]{3,0,1,2:T(8,128)(2,1)S(1)} fusion(bf16[4,1280,640]{2,1,0:T(8,128)(2,1)} %all-gather.5.cloned.1.call-done, bf16[4,640,1280]{2,1,0:T(8,128)(2,1)} %all-gather.3.cloned.1.call-done, bf16[32,5,4,640]{3,2,1,0:T(4,128)(2,1)S(1)} %all_to_all.10), kind=kOutput, calls=%fused_computation.22 | convolution fusion | flops 2104934400 | bytes 14745600 | tf_op jit(solution)/shard_map/scef,efw->scew/dot_general | solution.py:22
  139.7 1.3 copy.78
  141.0 5.0 %all-to-all-start.1 = ((bf16[32,5,4,640]{3,2,1,0:T(4,128)(2,1)}), bf16[32,5,4,640]{3,2,1,0:T(4,128)(2,1)S(1)}, u32[]{:S(2)}, u32[]{:S(2)}) async-start(bf16[32,5,4,640]{3,2,1,0:T(4,128)(2,1)} %copy.78), calls=%async_computation.1 | async-start | bytes 1638400 | tf_op jit(solution)/shard_map/all_to_all | solution.py:121
  146.0 0.2 convert_element_type.80
  146.1 0.1 copy.75
  146.3 0.2 reshape.171
  146.6 0.1 iota_compare_fusion.8
  146.7 0.3 fusion.76
  147.0 4.8 %fusion.75 = (f32[32,4,5]{2,1,0:T(4,128)S(1)}, f32[32,4,5,128]{3,2,1,0:T(8,128)S(1)}) fusion(bf16[32,4,5,128]{3,2,1,0:T(8,128)(2,1)S(1)} %reshape.171, pred[32,128]{1,0:T(8,128)(4,1)S(1)} %iota_compare_fusion.8, bf16[32,128,512]{2,1,0:T(8,128)(2,1)} %param.21), kind=kOutput, calls=%fused_computation.90 | convolution fusion | flops 21216640 | bytes 4692480 | tf_op jit(solution)/shard_map/tgqd,tjgd->tgqj/dot_general | solution.py:37
  151.8 0.4 fusion.49
  152.3 1.3 fusion.37
  153.6 0.1 reshape.175
  153.7 0.2 fusion.56
  153.9 0.2 select_reduce_fusion
  154.1 79.7 %all-to-all-done.1 = bf16[32,5,4,640]{3,2,1,0:T(4,128)(2,1)S(1)} async-done(((bf16[32,5,4,640]{3,2,1,0:T(4,128)(2,1)}), bf16[32,5,4,640]{3,2,1,0:T(4,128)(2,1)S(1)}, u32[]{:S(2)}, u32[]{:S(2)}) %all-to-all-start.1) | async-done | bytes 819232 | tf_op jit(solution)/shard_map/all_to_all | solution.py:121
  233.8 0.2 reshape.188
  234.0 0.5 fusion.40
  234.5 0.8 add_convert_fusion
  (35 shorter events, 0.4 us)
Async XLA Ops:
  7.2 146.5 %copy-start = (bf16[640,128]{1,0:T(8,128)(2,1)S(1)}, bf16[640,128]{1,0:T(8,128)(2,1)}, u32[]{:S(2)}) copy-start(bf16[640,128]{1,0:T(8,128)(2,1)} %param.14) | copy-start | bytes 491524
  7.2 1.6 copy-start.1
  7.2 1.9 copy-start.5
  7.2 1.9 copy-start.6
  7.2 124.8 %all-gather.3.cloned.1.call-start = ((), (), s32[]{:S(2)}) async-start(), calls=%async_computation.2 | async-start | bytes 9830400 | tf_op jit(solution)/shard_map/all_gather | solution.py:113
  8.0 124.0 %all-gather.5.cloned.1.call-start = ((), (), s32[]{:S(2)}) async-start(), calls=%async_computation.3 | async-start | bytes 9830400 | tf_op jit(solution)/shard_map/all_gather | solution.py:114
  132.0 14.3 %copy-start.2 = (bf16[32,2560]{1,0:T(8,128)(2,1)S(1)}, bf16[32,2560]{1,0:T(8,128)(2,1)}, u32[]{:S(2)}) copy-start(bf16[32,2560]{1,0:T(8,128)(2,1)} %param.18) | copy-start | bytes 491524
  132.0 14.5 %copy-start.3 = (bf16[32,512]{1,0:T(8,128)(2,1)S(1)}, bf16[32,512]{1,0:T(8,128)(2,1)}, u32[]{:S(2)}) copy-start(bf16[32,512]{1,0:T(8,128)(2,1)} %param.19) | copy-start | bytes 98308
  132.0 14.6 %copy-start.4 = (bf16[32,512]{1,0:T(8,128)(2,1)S(1)}, bf16[32,512]{1,0:T(8,128)(2,1)}, u32[]{:S(2)}) copy-start(bf16[32,512]{1,0:T(8,128)(2,1)} %param.20) | copy-start | bytes 98308
  132.0 14.6 %copy-start.7 = (s32[32]{0:T(128)S(1)}, s32[32]{0:T(128)}, u32[]{:S(2)}) copy-start(s32[32]{0:T(128)} %param.23) | copy-start | bytes 388
  141.0 92.8 %all-to-all-start.1 = ((bf16[32,5,4,640]{3,2,1,0:T(4,128)(2,1)}), bf16[32,5,4,640]{3,2,1,0:T(4,128)(2,1)S(1)}, u32[]{:S(2)}, u32[]{:S(2)}) async-start(bf16[32,5,4,640]{3,2,1,0:T(4,128)(2,1)} %copy.78), calls=%async_computation.1 | async-start | bytes 1638400 | tf_op jit(solution)/shard_map/all_to_all | solution.py:121
  146.6 5.7 %copy-start.8 = (bf16[32,128,512]{2,1,0:T(8,128)(2,1)S(1)}, bf16[32,128,512]{2,1,0:T(8,128)(2,1)}, u32[]{:S(2)}) copy-start(bf16[32,128,512]{2,1,0:T(8,128)(2,1)} %param.22) | copy-start | bytes 12582916
Sparse Core Ops, SparseCore 0:
  9.9 47.5 all-gather.2
  59.3 35.3 all-gather.4
where the time goes:
time: 243 us; the launch traced here: 242 us
  blocking collectives  121 us (50%)
  waiting for transfers between devices  81.2 us (33%)
  matrix products  15.5 us (6%)
  between operations  14.4 us (6%)
  starting transfers between devices  5.09 us (2%)
  local copies, waits for them, and re-layouts  3.06 us (1%)
    all_to_all x1, blocking collectives, per_device(): lax.all_to_all(outgoing, 'expert', split_axis=0, concat_axis=0, tiled=True)  121 us
    all_to_all x1, waiting for transfers between devices, per_device(): lax.all_to_all(result_rows, 'expert', split_axis=0, concat_axis=0, tiled=...  79.7 us
    dot_general x1, matrix products, expert_ffn(): jnp.einsum('scef,efw->scew', hidden, second_weight, preferred_element_typ...  7.63 us
    all_to_all x1, starting transfers between devices, per_device(): lax.all_to_all(result_rows, 'expert', split_axis=0, concat_axis=0, tiled=...  4.96 us
  transfers between devices with their start and end apart: 3, of which 1 were waited for; matrix products, arithmetic and copies ran while one was open for 4% of the time, Pallas kernels for 0%

commit v1 on v0

v1 whole, which is shorter than its diff:
```python
import functools
import math

import jax
import jax.numpy as jnp
from jax import lax
from jax.experimental import pallas as pl
from jax.experimental.pallas import tpu as pltpu
from jax.sharding import PartitionSpec as P

MESH = pl.DeviceIdType.MESH
F32 = jnp.float32
BF16 = jnp.bfloat16

SUB = 8
TOP = 2
CAP = 5
HD = 128
PER_GROUP = 5
CHUNK = 4
TOKEN_BLOCK = 8


def dot(a, b, dims=((1,), (0,))):
    return lax.dot_general(a, b, (dims, ((), ())), preferred_element_type=F32)


def gelu(v):
    return 0.5 * v * (1.0 + jnp.tanh(math.sqrt(2.0 / math.pi) * (v + 0.044715 * (v * v * v))))


def place(ring, delta):
    away = jnp.minimum(delta, ring - delta)
    behind = jnp.where(delta > ring // 2, 1, 0)
    return jnp.maximum(ring - 1 - 2 * away + behind, 0)


def delta_at(ring, pos):
    away = (ring - pos) // 2
    behind = jnp.where((pos % 2 == 0) & (pos > 0), 1, 0)
    return (ring + away - 2 * away * behind) % ring


def kernel(
    ring,
    res_ref,
    gain_ref,
    router_ref,
    ids_row_ref,
    ids_col_ref,
    query_ref,
    new_key_ref,
    new_value_ref,
    lengths_ref,
    w_in_ref,
    w_out_ref,
    keys_ref,
    values_ref,
    ctx_ref,
    moe_ref,
    normed,
    outbuf,
    inbuf,
    resbuf,
    retbuf,
    w_in,
    w_out,
    keys,
    values,
    acc,
    other,
    load_sem,
    pair_send,
    pair_recv,
    out_send,
    out_recv,
    ret_send,
    ret_recv,
):
    me = lax.axis_index("expert")
    core = lax.axis_index("mp")
    tokens, width = res_ref.shape
    sub_local = SUB // 2
    sub_width = width // sub_local
    own_rows = tokens * sub_local
    rows = 2 * own_rows
    experts = router_ref.shape[1]
    per_pair = 2 * CAP
    slots = ring * per_pair

    barrier = pltpu.get_barrier_semaphore()

    def greet(step, carry):
        pl.semaphore_signal(
            barrier, inc=1, device_id={"expert": (me + step) % ring}, device_id_type=MESH
        )
        return carry

    lax.fori_loop(1, ring, greet, 0)
    pl.semaphore_signal(barrier, inc=1, device_id={"mp": 1 - core}, device_id_type=MESH)

    loads = [
        pltpu.make_async_copy(w_in_ref.at[pl.ds(2 * core, 2)], w_in.at[0], load_sem.at[0]),
        pltpu.make_async_copy(w_out_ref.at[pl.ds(2 * core, 2)], w_out.at[0], load_sem.at[1]),
        pltpu.make_async_copy(keys_ref, keys, load_sem.at[2]),
        pltpu.make_async_copy(values_ref, values, load_sem.at[3]),
    ]
    for load in loads:
        load.start()

    for s in range(sub_local):
        cut = slice(s * sub_width, (s + 1) * sub_width)
        piece = res_ref[:, cut].astype(F32)
        meansq = jnp.mean(piece * piece, axis=-1, keepdims=True)
        scaled = piece * lax.rsqrt(meansq + 1e-06) * gain_ref[:, cut].astype(F32)
        normed[pl.ds(core * own_rows + s * tokens, tokens), :] = scaled.astype(BF16)

    def slot_of(ids, rank):
        delta = ((ids >> 2) - me + ring) % ring
        slot = place(ring, delta) * per_pair + rank.astype(jnp.int32) * 2 + (ids & 1)
        return jnp.where(((ids >> 1) & 1) == core, slot, -1)

    expert_rows = lax.broadcasted_iota(jnp.int32, (experts, rows), 0)
    named = [
        (expert_rows == ids_row_ref[k : k + 1, :]).astype(F32) for k in range(TOP)
    ]
    earlier = (
        lax.broadcasted_iota(jnp.int32, (rows, rows), 0)
        < lax.broadcasted_iota(jnp.int32, (rows, rows), 1)
    ).astype(BF16)
    before = dot((named[0] + named[1]).astype(BF16), earlier)
    slot_rows = lax.broadcasted_iota(jnp.int32, (slots, rows), 0)
    slot_row = [
        slot_of(ids_row_ref[k : k + 1, :], jnp.sum(named[k] * before, axis=0, keepdims=True))
        for k in range(TOP)
    ]
    dispatch = ((slot_rows == slot_row[0]) | (slot_rows == slot_row[1])).astype(BF16)

    pl.semaphore_wait(barrier, ring)

    def to_partner(src, dst, index):
        return pltpu.make_async_remote_copy(
            src_ref=src,
            dst_ref=dst,
            send_sem=pair_send.at[index],
            recv_sem=pair_recv.at[index],
            device_id={"mp": 1 - core},
            device_id_type=MESH,
        )

    mine = normed.at[pl.ds(core * own_rows, own_rows)]
    share = to_partner(mine, mine, 0)
    share.start()
    swaps = [
        to_partner(w_in_ref.at[pl.ds(2 * (1 - core), 2)], w_in.at[1], 1),
        to_partner(w_out_ref.at[pl.ds(2 * (1 - core), 2)], w_out.at[1], 2),
    ]
    for swap in swaps:
        swap.start()
    share.wait()

    outgoing = dot(dispatch, normed[...]).astype(BF16)
    outbuf[...] = outgoing.reshape(ring, CAP, 2, sub_width)
    inbuf[ring - 1] = outbuf[ring - 1]

    def outward(pos):
        return pltpu.make_async_remote_copy(
            src_ref=outbuf.at[pos],
            dst_ref=inbuf.at[pos],
            send_sem=out_send.at[pos],
            recv_sem=out_recv.at[pos],
            device_id={"expert": (me + delta_at(ring, pos)) % ring},
            device_id_type=MESH,
        )

    def homeward(pos):
        return pltpu.make_async_remote_copy(
            src_ref=resbuf.at[pos],
            dst_ref=retbuf.at[pos],
            send_sem=ret_send.at[pos],
            recv_sem=ret_recv.at[pos],
            device_id={"expert": (me + ring - delta_at(ring, pos)) % ring},
            device_id_type=MESH,
        )

    def send_out(pos, carry):
        outward(pos).start()
        return carry

    lax.fori_loop(0, ring - 1, send_out, 0)

    loads[2].wait()
    loads[3].wait()
    cache_len = keys.shape[1]
    kv_local = keys.shape[2] // HD
    score_scale = 1.0 / math.sqrt(HD)

    def attend(block, carry):
        contexts = []
        for b in range(TOKEN_BLOCK):
            context_of = []
            t = block * TOKEN_BLOCK + b
            scores, fresh = [], []
            for g in range(kv_local):
                cut = slice(g * HD, (g + 1) * HD)
                q = query_ref[t, g]
                scores.append(dot(q, keys[t, :, cut], ((1,), (1,))))
                key = new_key_ref[t, :, cut]
                fresh.append(jnp.sum(q.astype(F32) * key, axis=-1, keepdims=True))
            score = jnp.concatenate(scores, axis=0) * score_scale
            fresh_score = jnp.concatenate(fresh, axis=0) * score_scale
            usable = lax.broadcasted_iota(jnp.int32, score.shape, 1) < lengths_ref[t]
            score = jnp.where(usable, score, -1e30)
            row_max = jnp.maximum(jnp.max(score, axis=-1, keepdims=True), fresh_score)
            expo = jnp.where(usable, jnp.exp(score - row_max), 0.0)
            expo_new = jnp.exp(fresh_score - row_max)
            total = jnp.sum(expo, axis=-1, keepdims=True) + expo_new
            probs = (expo / total).astype(BF16)
            fresh_probs = (expo_new / total).astype(BF16).astype(F32)
            for g in range(kv_local):
                cut = slice(g * HD, (g + 1) * HD)
                part = slice(g * 8, (g + 1) * 8)
                context = dot(probs[part], values[t, :, cut])
                context_of.append(context + fresh_probs[part] * new_value_ref[t, :, cut])
            contexts.append(context_of)
        at = pl.ds(pl.multiple_of(block * TOKEN_BLOCK, TOKEN_BLOCK), TOKEN_BLOCK)
        for g in range(kv_local):
            for h in range(PER_GROUP):
                head = g * PER_GROUP + h
                lines = [context_of[g][h : h + 1] for context_of in contexts]
                ctx_ref[at, head * HD : (head + 1) * HD] = jnp.concatenate(lines, axis=0)
        return carry

    lax.fori_loop(0, tokens // TOKEN_BLOCK, attend, 0)

    loads[0].wait()
    loads[1].wait()
    for swap in swaps:
        swap.wait()

    even = lax.broadcasted_iota(jnp.int32, (CHUNK * per_pair, sub_width), 0) % 2 == 0

    def serve(chunk, carry):
        first = chunk * CHUNK
        for b in range(CHUNK):
            pos = first + b

            @pl.when(pos < ring - 1)
            def _():
                outward(pos).wait_recv()

        x = inbuf[pl.ds(first, CHUNK)].reshape(CHUNK * per_pair, sub_width)
        y = jnp.zeros((CHUNK * per_pair, sub_width), F32)
        for half in range(2):
            v = jnp.where(even, dot(x, w_in[half, 0]), dot(x, w_in[half, 1]))
            hidden = gelu(v).astype(BF16)
            none = jnp.zeros_like(hidden)
            y = y + dot(jnp.where(even, hidden, none), w_out[half, 0])
            y = y + dot(jnp.where(even, none, hidden), w_out[half, 1])
        resbuf[pl.ds(first, CHUNK)] = y.astype(BF16).reshape(CHUNK, CAP, 2, sub_width)
        for b in range(CHUNK):
            pos = first + b

            @pl.when(pos < ring - 1)
            def _():
                homeward(pos).start()

        return carry

    lax.fori_loop(0, ring // CHUNK, serve, 0)
    retbuf[ring - 1] = resbuf[ring - 1]

    expert_cols = lax.broadcasted_iota(jnp.int32, (rows, experts), 1)
    logits = dot(normed[...], router_ref[...])
    named = [(expert_cols == ids_col_ref[:, k : k + 1]).astype(F32) for k in range(TOP)]
    earlier = (
        lax.broadcasted_iota(jnp.int32, (rows, rows), 1)
        < lax.broadcasted_iota(jnp.int32, (rows, rows), 0)
    ).astype(BF16)
    before = dot(earlier, (named[0] + named[1]).astype(BF16))
    gate, slot_col = [], []
    for k in range(TOP):
        picked = jnp.sum(named[k] * logits, axis=-1, keepdims=True)
        gate.append(1.0 / (1.0 + jnp.exp(-picked)))
        rank = jnp.sum(named[k] * before, axis=-1, keepdims=True)
        slot_col.append(slot_of(ids_col_ref[:, k : k + 1], rank))
    gate_sum = gate[0] + gate[1]
    weight = [g / gate_sum for g in gate]

    groups = 4
    span = ring // groups
    for group in range(groups):
        first = group * span
        for pos in range(first, min(first + span, ring - 1)):
            homeward(pos).wait_recv()
        back = retbuf[first : first + span].reshape(span * per_pair, sub_width)
        cols = lax.broadcasted_iota(jnp.int32, (rows, span * per_pair), 1) + first * per_pair
        part = weight[0] * dot((cols == slot_col[0]).astype(BF16), back)
        part = part + weight[1] * dot((cols == slot_col[1]).astype(BF16), back)
        acc[...] = part if group == 0 else acc[...] + part

    hand = to_partner(acc.at[pl.ds((1 - core) * own_rows, own_rows)], other, 3)
    hand.start()

    def sent(pos, carry):
        outward(pos).wait_send()
        homeward(pos).wait_send()
        return carry

    lax.fori_loop(0, ring - 1, sent, 0)
    hand.wait()
    for s in range(sub_local):
        cut = slice(s * sub_width, (s + 1) * sub_width)
        own = acc[pl.ds(core * own_rows + s * tokens, tokens), :]
        moe_ref[:, cut] = own + other[s * tokens : (s + 1) * tokens, :]


def solution(mesh):
    ring = mesh.shape["expert"]

    def per_device(
        residual,
        norm_gain,
        router_weight,
        expert_ids,
        expert_in,
        expert_out,
        queries,
        new_keys,
        new_values,
        cache_keys,
        cache_values,
        lengths,
    ):
        tokens, width = residual.shape
        sub_width = router_weight.shape[0]
        rows = tokens * SUB
        kv_local = new_keys.shape[1] // HD
        half_hidden = expert_in.shape[2]
        ids_row = expert_ids.transpose(2, 1, 0).reshape(TOP, rows)
        ids_col = expert_ids.transpose(1, 0, 2).reshape(rows, TOP)
        query = jnp.pad(
            queries.reshape(tokens, kv_local, PER_GROUP, HD),
            ((0, 0), (0, 0), (0, 8 - PER_GROUP), (0, 0)),
        )
        vmem = pl.BlockSpec(memory_space=pltpu.VMEM)
        hbm = pl.BlockSpec(memory_space=pl.ANY)
        smem = pl.BlockSpec(memory_space=pltpu.SMEM)
        block = (ring, CAP, 2, sub_width)
        context, moe = pl.pallas_call(
            functools.partial(kernel, ring),
            out_shape=[jax.ShapeDtypeStruct((tokens, width), F32)] * 2,
            in_specs=[vmem] * 8 + [smem] + [hbm] * 4,
            out_specs=[vmem] * 2,
            scratch_shapes=[
                pltpu.VMEM((rows, sub_width), BF16),
                pltpu.VMEM(block, BF16),
                pltpu.VMEM(block, BF16),
                pltpu.VMEM(block, BF16),
                pltpu.VMEM(block, BF16),
                pltpu.VMEM((2, 2, sub_width, half_hidden), BF16),
                pltpu.VMEM((2, 2, half_hidden, sub_width), BF16),
                pltpu.VMEM(cache_keys.shape, BF16),
                pltpu.VMEM(cache_values.shape, BF16),
                pltpu.VMEM((rows, sub_width), F32),
                pltpu.VMEM((rows // 2, sub_width), F32),
                pltpu.SemaphoreType.DMA((4,)),
                pltpu.SemaphoreType.DMA((4,)),
                pltpu.SemaphoreType.DMA((4,)),
                pltpu.SemaphoreType.DMA((ring,)),
                pltpu.SemaphoreType.DMA((ring,)),
                pltpu.SemaphoreType.DMA((ring,)),
                pltpu.SemaphoreType.DMA((ring,)),
            ],
            compiler_params=pltpu.CompilerParams(collective_id=0, has_side_effects=True),
            name="step",
        )(
            residual,
            norm_gain.reshape(1, width),
            router_weight,
            ids_row,
            ids_col,
            query,
            new_keys.astype(F32).reshape(tokens, 1, -1),
            new_values.astype(F32).reshape(tokens, 1, -1),
            lengths,
            expert_in,
            expert_out,
            cache_keys,
            cache_values,
        )
        attention = context.astype(BF16)
        mixed = (residual.astype(F32) + context + moe).astype(BF16)
        return attention, mixed

    both = ("groups", "expert")
    placed = (
        P(both, "mp"),
        P("mp"),
        P(),
        P(both, None, None),
        P("expert", None, "mp"),
        P("expert", "mp", None),
        P(both, "mp"),
        P(both, "mp"),
        P(both, "mp"),
        P(both, None, "mp"),
        P(both, None, "mp"),
        P(both),
    )
    return jax.shard_map(
        per_device,
        mesh=mesh,
        in_specs=placed,
        out_specs=(P(both, "mp"), P(both, "mp")),
        check_vma=False,
    )
```

time: 243 us -> 124 us (0.51)
  blocking collectives: 121 us -> 0 us
  Pallas kernels: 0 us -> 112 us
  waiting for transfers between devices: 81.2 us -> 0 us
  matrix products: 15.5 us -> 0 us
  between operations: 14.4 us -> 0.65 us
  local copies, waits for them, and re-layouts: 3.06 us -> 8.86 us
  starting transfers between devices: 5.09 us -> 0 us
    all_to_all x1 -> x0, blocking collectives: 121 us -> none  [per_device(): lax.all_to_all(outgoing, 'expert', split_axis=0, concat_axis=0, tiled=True)]
    pallas_call x0 -> x1, Pallas kernels: none -> 112 us  [per_device(): pl.pallas_call(functools.partial(kernel, ring), out_shape=[jax.ShapeDtype...]
    all_to_all x1 -> x0, waiting for transfers between devices: 79.7 us -> none  [per_device(): lax.all_to_all(result_rows, 'expert', split_axis=0, concat_axis=0, tiled=...]
    dot_general x8 -> x0, matrix products: 15.5 us -> none  [the longest x1 7.63 us: expert_ffn(): jnp.einsum('scef,efw->scew', hidden, second_weight, preferred_element_typ...]
    reshape x8 -> x5, local copies, waits for them, and re-layouts: 0.96 us -> 5.93 us  [the longest x1 1.43 us: per_device(): new_values.astype(F32).reshape(tokens, 1, -1)]
    all_to_all x1 -> x0, starting transfers between devices: 4.96 us -> none  [per_device(): lax.all_to_all(result_rows, 'expert', split_axis=0, concat_axis=0, tiled=...]
  transfers between devices with their start and end apart: 3 -> 0, of which waited for: 1 -> 0; matrix products, arithmetic and copies ran while one was open for 4% -> 0% of each run, Pallas kernels for 0% -> 0%
where the time goes in v1:
time: 124 us
  Pallas kernels  112 us (90%)
  local copies, waits for them, and re-layouts  8.86 us (7%)
  other arithmetic  1.95 us (2%)
    pallas_call x1, Pallas kernels, per_device(): pl.pallas_call(functools.partial(kernel, ring), out_shape=[jax.ShapeDtype...  112 us

profile of v1, /device:TPU:37, one launch (start us, length us, event | category | flops | bytes accessed | tf_op | source)
XLA Modules:
  0.0 123.8 jit_solution(12434934949088157094)
XLA Ops:
  0.6 0.7 copy.16
  1.3 0.7 reshape.27.ids_row_ref
  2.0 1.3 %reshape.26.gain_ref = bf16[1,2560]{1,0:T(2,128)(2,1)} reshape(bf16[2560]{0:T(1024)(128)(2,1)} %param.13) | data formatting | bytes 10240 | tf_op jit(solution)/shard_map/reshape | solution.py:379
  3.3 1.4 %reshape.35.new_key_ref = f32[32,1,512]{2,1,0:T(1,128)} reshape(bf16[32,512]{1,0:T(8,128)(2,1)} %param.19) | data formatting | bytes 98304 | tf_op jit(solution)/shard_map/reshape | solution.py:384
  4.7 1.4 %reshape.37.new_value_ref = f32[32,1,512]{2,1,0:T(1,128)} reshape(bf16[32,512]{1,0:T(8,128)(2,1)} %param.20) | data formatting | bytes 98304 | tf_op jit(solution)/shard_map/reshape | solution.py:385
  6.1 1.5 %copy.17 = s32[8,32,2]{2,1,0:T(8,128)} copy(s32[8,32,2]{1,2,0:T(2,128)} %bitcast.5) | data formatting | bytes 4096 | tf_op jit(solution)/shard_map/transpose | solution.py:341
  7.6 1.1 reshape.29
  8.7 0.7 pad.4.query_ref
  9.5 0.0 copy-start
  9.5 112.3 %step.1 = (f32[32,2560]{1,0:T(8,128)}, f32[32,2560]{1,0:T(8,128)}) custom-call(bf16[32,2560]{1,0:T(8,128)(2,1)} %res_ref.1, bf16[1,2560]{1,0:T(2,128)(2,1)} %reshape.26.gain_ref, bf16[640,128]{1,0:T(8,128)(2,1)} %router_ref.1, s32[2,256]{1,0:T(2,128)} %reshape.27.ids_row_ref, s32[256,2]{1,0:T(8,128)} %bitcast.3, bf16[32,4,8,128]{3,2,1,0:T(8,128)(2,1)} %pad.4.query_ref, ...), custom_call_target="tpu_custom_call" | custom-call | tf_op jit(solution)/shard_map/step/pallas_call | solution.py:350
  121.8 0.0 copy-done
  121.8 1.9 %add_convert_fusion = (bf16[32,2560]{1,0:T(8,128)(2,1)}, bf16[32,2560]{1,0:T(8,128)(2,1)}) fusion(f32[32,2560]{1,0:T(8,128)} %get-tuple-element.5, f32[32,2560]{1,0:T(8,128)} %get-tuple-element.4, bf16[32,2560]{1,0:T(8,128)(2,1)S(1)} %copy-done), kind=kLoop, calls=%fused_computation | loop fusion | flops 409600 | bytes 1146880 | tf_op jit(solution)/shard_map/convert_element_type | solution.py:393
Async XLA Ops:
  9.5 112.3 %copy-start = (bf16[32,2560]{1,0:T(8,128)(2,1)S(1)}, bf16[32,2560]{1,0:T(8,128)(2,1)}, u32[]{:S(2)}) copy-start(bf16[32,2560]{1,0:T(8,128)(2,1)} %res_ref.1) | copy-start | bytes 491524
